TPU v7x, 32 devices: a whole 2x2x4 slice. The times are simulated.
32 devices in a mesh: pair: 4 (over y, x), aux: 8 (over z, core).
Axes of the slice: x: 2, y: 2, z: 4, core: 2. Of those that a mesh axis runs over, the one named last changes fastest.
Arguments:
- amplitudes: bfloat16 [4, 512, 512], P('pair', 'aux'), may hold values from -6 to 6
- factors: bfloat16 [4096, 512, 512], P('aux', 'pair'), may hold values from -0.03125 to 0.03125
- hole_weights: float32 [4, 4], replicated, may hold values from -3 to 3
- driver: float32 [4, 6, 512], P('pair', None, 'aux'), may hold values from -6 to 6
- eps_vir: float32 [512], replicated, may hold values from 0.5 to 3
- pair_energy: float32 [4], P('pair'), may hold values from -3 to -0.5
Outputs:
- residual: float32 [4, 6, 512], P('pair', None, 'aux')
- new_amps: float32 [4, 6, 512], P('pair', None, 'aux')
All inputs are finite; a program needn't handle non-finite values.
Results may differ from a plain program's by a relative error of at most 0.0003.
Values may be sent and summed in bfloat16 or wider, within the bound.
A program may use at most 192 MiB of HBM per device.

v0:
```python
import functools

import jax
import jax.numpy as jnp
from jax import lax
from jax.experimental import pallas as pl
from jax.experimental.pallas import tpu as pltpu
from jax.sharding import PartitionSpec as P

MESH = pl.DeviceIdType.MESH
F32 = jnp.float32
BF16 = jnp.bfloat16


def ring_order(n):
    side = 1
    while side * side < n:
        side += 1
    if side * side != n or side % 2:
        return list(range(n))
    order = []
    for row in range(side):
        cols = list(range(1, side))
        if row % 2:
            cols.reverse()
        if row == 0:
            cols = [0] + cols
        order += [row * side + col for col in cols]
    order += [row * side for row in range(side - 1, 0, -1)]
    return order


def lookup(index, table):
    value = jnp.int32(table[0])
    for at, entry in enumerate(table[1:], 1):
        value = jnp.where(index == at, jnp.int32(entry), value)
    return value


def kernel(
    n_pair, n_aux, rows, chunk, slots,
    amp_ref, win_ref, fac_ref,
    sum_ref, slab_ref,
    t_ref, w_ref, f_ref, h_ref, e_ref, part_ref, got_ref,
    f_sem, loc_sem, wl_sem, a_send, a_recv, z_send, z_recv, c_send, c_recv, w_send, w_recv, r_send, r_recv,
):
    width = amp_ref.shape[2]
    own_rows = amp_ref.shape[1]
    block = fac_ref.shape[1]
    chunks = w_ref.shape[0]
    pad = 8
    m = n_aux // 2
    i = lax.axis_index("pair")
    j = lax.axis_index("aux")
    z = j // 2
    core = lax.rem(j, 2)

    order = ring_order(n_pair)
    where = [order.index(k) for k in range(n_pair)]
    pos = lookup(i, where)
    right = lookup(i, [order[(where[k] + 1) % n_pair] for k in range(n_pair)])
    left = lookup(i, [order[(where[k] - 1) % n_pair] for k in range(n_pair)])

    def rows_of(at):
        return pl.ds(pl.multiple_of(at * own_rows, own_rows), own_rows)

    def load_factors(k):
        slot = lax.rem(k, slots)
        return pltpu.make_async_copy(
            fac_ref.at[pl.ds(pl.multiple_of(k * chunk, chunk), chunk)], f_ref.at[slot], f_sem.at[slot]
        )

    local = pltpu.make_async_copy(amp_ref.at[0], t_ref.at[i, rows_of(j)], loc_sem)
    local.start()

    def a_copy(peer, source):
        return pltpu.make_async_remote_copy(
            src_ref=amp_ref.at[0], dst_ref=t_ref.at[source, rows_of(j)],
            send_sem=a_send.at[peer], recv_sem=a_recv.at[source],
            device_id=(peer, j), device_id_type=MESH,
        )

    for step in range(1, n_pair):
        peer = lax.rem(i + step, n_pair)
        a_copy(peer, i).start()

    def w_load(k):
        return pltpu.make_async_copy(win_ref.at[k], w_ref.at[k], wl_sem.at[k])

    def w_copy(k, target):
        return pltpu.make_async_remote_copy(
            src_ref=w_ref.at[k], dst_ref=w_ref.at[k],
            send_sem=w_send.at[k], recv_sem=w_recv.at[k],
            device_id=(target, j), device_id_type=MESH,
        )

    def target_of(k):
        return jnp.where(lax.rem(k, 2) == 0, right, left)

    def distance(k):
        return jnp.where(lax.rem(k, 2) == 0, pos, lax.rem(n_pair - pos, n_pair))

    @pl.when(pos == 0)
    def _():
        @pl.loop(0, chunks)
        def _(k):
            w_load(k).start()

        @pl.loop(0, chunks)
        def _(k):
            w_load(k).wait()
            w_copy(k, target_of(k)).start()

    for k in range(slots):
        load_factors(k).start()

    e_row = lax.broadcasted_iota(jnp.int32, e_ref.shape, 0)
    e_col = lax.broadcasted_iota(jnp.int32, e_ref.shape, 1)
    hit = (e_col == (e_row // pad) * rows + e_row % pad) & (e_row % pad < rows)
    e_ref[...] = jnp.where(hit, 1.0, 0.0).astype(BF16)

    local.wait()
    for step in range(1, n_pair):
        source = lax.rem(i + n_pair - step, n_pair)
        a_copy(i, source).wait_recv()

    def z_copy(peer, source):
        return pltpu.make_async_remote_copy(
            src_ref=t_ref.at[:, rows_of(j)], dst_ref=t_ref.at[:, rows_of(source * 2 + core)],
            send_sem=z_send.at[peer], recv_sem=z_recv.at[source],
            device_id=(i, peer * 2 + core), device_id_type=MESH,
        )

    def c_copy(source, own):
        held = rows_of(source * 2 + own)
        return pltpu.make_async_remote_copy(
            src_ref=t_ref.at[:, held], dst_ref=t_ref.at[:, held],
            send_sem=c_send.at[source], recv_sem=c_recv.at[source],
            device_id=(i, z * 2 + 1 - core), device_id_type=MESH,
        )

    for step in range(1, m):
        z_copy(lax.rem(z + step, m), z).start()
    c_copy(z, core).start()
    for step in range(1, m):
        source = lax.rem(z + m - step, m)
        z_copy(z, source).wait_recv()
        c_copy(source, core).start()

    def handle(k):
        dist = distance(k)
        w_copy(k, target_of(k)).wait_recv()

        @pl.when(dist < n_pair - 1)
        def _():
            w_copy(k, target_of(k)).start()

    def look(k):
        return 2 * (n_pair - 1 - distance(k))

    @pl.when(pos > 0)
    def _():
        @pl.loop(0, chunks)
        def _(k):
            @pl.when(k < look(k))
            def _():
                handle(k)

    for source in range(m):
        c_copy(source, 1 - core).wait_recv()

    part_ref[...] = jnp.zeros_like(part_ref)

    @pl.loop(0, chunks)
    def _(k):
        ahead = k + look(k)

        @pl.when((pos > 0) & (ahead < chunks))
        def _():
            handle(ahead)

        wide = jnp.dot(e_ref[...], w_ref[k], preferred_element_type=F32).astype(BF16)
        for p in range(0, n_pair, 2):
            two = [
                jnp.dot(wide, t_ref[p + at], preferred_element_type=F32).reshape(chunk, pad, width)
                for at in range(2)
            ]
            h_ref[:, p * pad : (p + 2) * pad, :] = jnp.concatenate(two, axis=1).astype(BF16)
        load_factors(k).wait()
        slot = lax.rem(k, slots)

        def add(q, total):
            return total + lax.dot_general(
                f_ref[slot, q], h_ref[q], (((1,), (1,)), ((), ())), preferred_element_type=F32
            )

        total = lax.fori_loop(0, chunk, add, jnp.zeros((block, n_pair * pad), F32), unroll=8)
        part_ref[...] += total.T.reshape(n_pair, pad, block)

        @pl.when(k + slots < chunks)
        def _():
            load_factors(k + slots).start()

    ratio = n_aux // n_pair

    def r_copy(p, t, source, to):
        return pltpu.make_async_remote_copy(
            src_ref=part_ref.at[p], dst_ref=got_ref.at[source],
            send_sem=r_send.at[p * ratio + t], recv_sem=r_recv.at[source],
            device_id=to, device_id_type=MESH,
        )

    for p in range(n_pair):
        for t in range(ratio):
            column = i * ratio + t
            mine = (i == p) & (j == column)

            @pl.when(mine)
            def _():
                got_ref[j] = part_ref[p]

            @pl.when(jnp.logical_not(mine))
            def _():
                r_copy(p, t, j, (jnp.int32(p), column)).start()

    slab_ref[...] = t_ref[:, 0:16, :]
    column_owner = j // ratio
    for source in range(n_aux):
        @pl.when(jnp.logical_not((column_owner == i) & (j == source)))
        def _():
            r_copy(0, 0, source, (i, j)).wait_recv()

    total = got_ref[0]
    for source in range(1, n_aux):
        total = total + got_ref[source]
    sum_ref[...] = total

    for p in range(n_pair):
        for t in range(ratio):
            column = i * ratio + t

            @pl.when(jnp.logical_not((i == p) & (j == column)))
            def _():
                r_copy(p, t, j, (jnp.int32(p), column)).wait_send()
    for step in range(1, n_pair):
        a_copy(lax.rem(i + step, n_pair), i).wait_send()
    for step in range(1, m):
        z_copy(lax.rem(z + step, m), z).wait_send()
    for source in range(m):
        c_copy(source, core).wait_send()

    @pl.loop(0, chunks)
    def _(k):
        @pl.when(distance(k) < n_pair - 1)
        def _():
            w_copy(k, target_of(k)).wait_send()


def per_device(n_pair, n_aux, amplitudes, factors, hole_weights, driver, eps_vir, pair_energy):
    rows, columns = driver.shape[1:]
    depth, block, width = factors.shape
    own_rows = amplitudes.shape[1]
    chunk = min(32, depth)
    chunks = depth // chunk
    slots = min(8, chunks)
    window = factors[:, :rows, :].reshape(chunks, chunk * rows, width)
    pad = 8
    m = n_aux // 2
    ratio = n_aux // n_pair
    vmem = pl.BlockSpec(memory_space=pltpu.VMEM)
    hbm = pl.BlockSpec(memory_space=pl.ANY)
    dma = pltpu.SemaphoreType.DMA
    summed, slab = pl.pallas_call(
        functools.partial(kernel, n_pair, n_aux, rows, chunk, slots),
        out_shape=(
            jax.ShapeDtypeStruct((pad, block), F32),
            jax.ShapeDtypeStruct((n_pair, 16, width), BF16),
        ),
        in_specs=[hbm, hbm, hbm],
        out_specs=(vmem, vmem),
        scratch_shapes=[
            pltpu.VMEM((n_pair, n_aux * own_rows, width), BF16),
            pltpu.VMEM((chunks, chunk * rows, width), BF16),
            pltpu.VMEM((slots, chunk, block, width), BF16),
            pltpu.VMEM((chunk, n_pair * pad, width), BF16),
            pltpu.VMEM((chunk * pad, chunk * rows), BF16),
            pltpu.VMEM((n_pair, pad, block), F32),
            pltpu.VMEM((n_aux, pad, block), F32),
            dma((slots,)),
            dma,
            dma((chunks,)),
            dma((n_pair,)),
            dma((n_pair,)),
            dma((m,)),
            dma((m,)),
            dma((m,)),
            dma((m,)),
            dma((chunks,)),
            dma((chunks,)),
            dma((n_pair * ratio,)),
            dma((n_aux,)),
        ],
        compiler_params=pltpu.CompilerParams(has_side_effects=True, vmem_limit_bytes=60 * 1024 * 1024),
    )(amplitudes, window, factors)

    pair_index = lax.axis_index("pair")
    aux_index = lax.axis_index("aux")
    start = aux_index * columns
    slab_cols = lax.dynamic_slice_in_dim(slab[:, :rows], start, columns, 2).astype(F32)
    weights = lax.dynamic_slice_in_dim(hole_weights, pair_index, 1, 0)[0]
    hole = weights[0] * slab_cols[0]
    for k in range(1, n_pair):
        hole = hole + weights[k] * slab_cols[k]
    particle = lax.dynamic_slice_in_dim(summed[:rows], lax.rem(aux_index, ratio) * columns, columns, 1)
    residual = driver + (particle + hole)[None]
    amp_cols = lax.dynamic_slice_in_dim(slab_cols, pair_index, 1, 0)
    eps_cols = lax.dynamic_slice_in_dim(eps_vir, start, columns, 0)
    denominator = eps_vir[:rows][None, :, None] + eps_cols[None, None, :] - pair_energy[:, None, None]
    return residual, amp_cols - residual / denominator


def solution(mesh):
    return jax.shard_map(
        functools.partial(per_device, mesh.shape["pair"], mesh.shape["aux"]),
        mesh=mesh,
        in_specs=(
            P("pair", "aux", None),
            P("aux", "pair", None),
            P(),
            P("pair", None, "aux"),
            P(),
            P("pair"),
        ),
        out_specs=(P("pair", None, "aux"), P("pair", None, "aux")),
        check_vma=False,
    )
```

profile of v0, /device:TPU:13, one launch (start us, length us, event | category | flops | bytes accessed | tf_op | source)
XLA Modules:
  0.0 115.5 jit_solution(12586330009218189944)
XLA Ops:
  0.6 0.0 copy-start
  0.6 4.4 %slice.40 = bf16[512,6,512]{2,1,0:T(8,128)(2,1)} slice(bf16[512,128,512]{2,1,0:T(8,128)(2,1)} %fac_ref.1), slice={[0:512], [0:6], [0:512]} | slice | bytes 6291456 | tf_op jit(solution)/shard_map/slice | solution.py:266
  5.0 6.4 %reshape.81.win_ref = bf16[16,192,512]{2,1,0:T(8,128)(2,1)} reshape(bf16[512,6,512]{2,1,0:T(8,128)(2,1)} %slice.40) | data formatting | bytes 6291456 | tf_op jit(solution)/shard_map/reshape | solution.py:266
  11.5 0.0 copy-start.2
  11.5 0.0 copy-start.1
  11.5 0.0 slice-start
  11.5 97.4 %shard_map.77 = (f32[8,128]{1,0:T(8,128)}, bf16[4,16,512]{2,1,0:T(8,128)(2,1)}) custom-call(bf16[1,64,512]{2,1,0:T(8,128)(2,1)} %amp_ref.1, bf16[16,192,512]{2,1,0:T(8,128)(2,1)} %reshape.81.win_ref, bf16[512,128,512]{2,1,0:T(8,128)(2,1)} %fac_ref.1), custom_call_target="tpu_custom_call" | custom-call | tf_op jit(solution)/shard_map/pallas_call | solution.py:273
  108.8 0.8 slice.43
  109.6 0.1 dynamic-slice_convert_fusion
  110.3 0.0 copy-done.2
  110.3 0.1 dynamic_slice.19
  110.4 0.0 copy-done
  110.4 0.7 fusion.8
  111.1 0.0 copy-done.1
  111.1 0.0 slice-done
  111.1 3.3 %divide_subtract_fusion = (f32[1,6,64]{2,1,0:T(8,128)S(1)}, f32[1,6,64]{2,1,0:T(8,128)S(1)}) fusion(f32[4,6,64]{2,1,0:T(8,128)S(1)} %dynamic-slice_convert_fusion, s32[]{:T(128)S(6)} %select_n.12, f32[]{:T(128)} %bitcast.20, f32[64]{0:T(128)S(1)} %dynamic_slice.19, f32[6]{0:T(128)S(1)} %slice-done, f32[]{:T(128)} %bitcast.3, f32[]{:T(128)} %bitcast.2, ...), kind=kLoop, calls=%fused_computation.12 | loop fusion | flops 4992 | bytes 14132 | tf_op jit(solution)/shard_map/sub | solution.py:319
  114.4 0.6 copy.12
  114.9 0.6 copy.13
  (1 shorter events, 0.0 us)
Async XLA Ops:
  0.6 109.8 %copy-start = (f32[4,4]{1,0:T(4,128)S(1)}, f32[4,4]{1,0:T(4,128)}, u32[]{:S(2)}) copy-start(f32[4,4]{1,0:T(4,128)} %param.8) | copy-start | bytes 196
  11.5 98.9 %copy-start.2 = (f32[512]{0:T(512)S(1)}, f32[512]{0:T(512)}, u32[]{:S(2)}) copy-start(f32[512]{0:T(512)} %param.10) | copy-start | bytes 6148
  11.5 99.6 %copy-start.1 = (f32[1,6,64]{2,0,1:T(1,128)S(1)}, f32[1,6,64]{2,0,1:T(1,128)}, u32[]{:S(2)}) copy-start(f32[1,6,64]{2,0,1:T(1,128)} %param.9) | copy-start | bytes 4612
  11.5 99.6 %slice-start = ((f32[512]{0:T(512)}), f32[6]{0:T(128)S(1)}, s32[]{:S(2)}) async-start(f32[512]{0:T(512)} %param.10), calls=%async_computation | async-start | bytes 1024 | tf_op jit(solution)/shard_map/slice | solution.py:318
where the time goes:
time: 116 us
  Pallas kernels  97.4 us (84%)
  local copies, waits for them, and re-layouts  13.5 us (12%)
  other arithmetic  3.34 us (3%)
  between operations  1.31 us (1%)
    pallas_call x1, Pallas kernels, per_device(): pl.pallas_call(functools.partial(kernel, n_pair, n_aux, rows, chunk, slot...  97.4 us
    reshape x1, local copies, waits for them, and re-layouts, per_device(): window = factors[:, :rows, :].reshape(chunks, chunk * rows, width)  6.4 us
    slice x1, local copies, waits for them, and re-layouts, per_device(): window = factors[:, :rows, :].reshape(chunks, chunk * rows, width)  4.4 us
    sub x1, other arithmetic, per_device(): return (residual, amp_cols - residual / denominator)  3.26 us

commit v1 on v0

v1 whole, which is shorter than its diff:
```python
import functools

import jax
import jax.numpy as jnp
from jax import lax
from jax.experimental import pallas as pl
from jax.experimental.pallas import tpu as pltpu
from jax.sharding import PartitionSpec as P

MESH = pl.DeviceIdType.MESH
F32 = jnp.float32
BF16 = jnp.bfloat16
PAD = 8
SPLIT = 2
LEAD = 2
STAGES = (-2, 1, 2)
PACE = (9, 10)


def ring_order(n):
    side = 1
    while side * side < n:
        side += 1
    if side * side != n or side % 2:
        return list(range(n))
    order = []
    for row in range(side):
        cols = list(range(1, side))
        if row % 2:
            cols.reverse()
        if row == 0:
            cols = [0] + cols
        order += [row * side + col for col in cols]
    order += [row * side for row in range(side - 1, 0, -1)]
    return order


def lookup(index, table):
    value = jnp.int32(table[0])
    for at, entry in enumerate(table[1:], 1):
        value = jnp.where(index == at, jnp.int32(entry), value)
    return value


def kernel(
    n_pair, n_aux, rows, columns, chunk, unit, slots, early,
    amp_ref, fac_ref, hole_ref, driver_ref, eps_ref, eps_row_ref, energy_ref,
    res_ref, new_ref,
    t_ref, w8_ref, w_ref, f_ref, h_ref, part_ref, flip_ref, send_ref, got_ref, keep_ref, pick_ref,
    f_sem, loc_sem, w8_sem, o_send, o_recv, y_send, y_recv, m_send, m_recv,
    z_send, z_recv, c_send, c_recv, w_send, w_recv, r_send, r_recv,
):
    width = amp_ref.shape[2]
    own_rows = amp_ref.shape[1]
    depth, block = fac_ref.shape[:2]
    chunks = depth // chunk
    units = depth // unit
    per = chunk // unit
    steps = units // 2
    m = n_aux // 2
    half = m // 2
    i = lax.axis_index("pair")
    j = lax.axis_index("aux")
    z = j // 2
    core = lax.rem(j, 2)
    mirror = lax.rem(z + half, m)
    base = (z // half) * half
    far = (mirror // half) * half

    order = ring_order(n_pair)
    where = [order.index(k) for k in range(n_pair)]
    pos = lookup(i, where)
    right = lookup(i, [order[(where[k] + 1) % n_pair] for k in range(n_pair)])
    left = lookup(i, [order[(where[k] - 1) % n_pair] for k in range(n_pair)])

    def rows_of(at):
        return pl.ds(pl.multiple_of(at * own_rows, own_rows), own_rows)

    def load_factors(k):
        slot = lax.rem(k, slots)
        return pltpu.make_async_copy(
            fac_ref.at[pl.ds(pl.multiple_of(k * chunk, chunk), chunk)], f_ref.at[slot], f_sem.at[slot]
        )

    def w8_load(k):
        return pltpu.make_async_copy(
            fac_ref.at[pl.ds(pl.multiple_of(k * chunk, chunk), chunk), pl.ds(0, PAD)], w8_ref.at[k], w8_sem.at[k]
        )

    def o_copy(peer, source):
        return pltpu.make_async_remote_copy(
            src_ref=amp_ref.at[0], dst_ref=t_ref.at[source, rows_of(j)],
            send_sem=o_send.at[peer], recv_sem=o_recv.at[source],
            device_id=(peer, j), device_id_type=MESH,
        )

    def mirror_copy(target, source):
        return pltpu.make_async_remote_copy(
            src_ref=amp_ref.at[0], dst_ref=t_ref.at[i, rows_of(source * 2 + core)],
            send_sem=y_send, recv_sem=y_recv,
            device_id=(i, target * 2 + core), device_id_type=MESH,
        )

    def m_copy(peer, source):
        held = rows_of(mirror * 2 + core)
        return pltpu.make_async_remote_copy(
            src_ref=t_ref.at[source, held], dst_ref=t_ref.at[source, held],
            send_sem=m_send.at[peer], recv_sem=m_recv.at[source],
            device_id=(peer, j), device_id_type=MESH,
        )

    def z_copy(target, group):
        held = rows_of(group * 2 + core)
        at = lax.rem(target + half - base, half) + jnp.where(group // half == z // half, 0, half)
        return pltpu.make_async_remote_copy(
            src_ref=t_ref.at[:, held], dst_ref=t_ref.at[:, held],
            send_sem=z_send.at[at], recv_sem=z_recv.at[group],
            device_id=(i, target * 2 + core), device_id_type=MESH,
        )

    def c_copy(group, own):
        held = rows_of(group * 2 + own)
        return pltpu.make_async_remote_copy(
            src_ref=t_ref.at[:, held], dst_ref=t_ref.at[:, held],
            send_sem=c_send.at[group], recv_sem=c_recv.at[group],
            device_id=(i, z * 2 + 1 - core), device_id_type=MESH,
        )

    def w_copy(u, target):
        return pltpu.make_async_remote_copy(
            src_ref=w_ref.at[u], dst_ref=w_ref.at[u],
            send_sem=w_send.at[u], recv_sem=w_recv.at[u],
            device_id=(target, j), device_id_type=MESH,
        )

    targets = (right, left)
    distances = (pos, lax.rem(n_pair - pos, n_pair))

    def squeeze(k):
        w8_load(k).wait()
        wide = w8_ref[k].reshape(chunk * PAD, width)
        tight = jnp.dot(pick_ref[...], wide, preferred_element_type=F32).astype(BF16)
        w_ref[pl.ds(k * per, per)] = tight.reshape(per, unit * rows, width)

    def send_units(k):
        for at in range(per):
            w_copy(k * per + at, targets[at % 2]).start()

    near = jnp.where(distances[0] <= distances[1], 0, 1)

    def distance(d):
        return jnp.where(d == 0, distances[0], distances[1])

    def handle(first, last):
        @pl.when(pos > 0)
        def _():
            for d in (near, 1 - near):
                target = jnp.where(d == 0, right, left)

                @pl.loop(first(d), last(d))
                def _(s):
                    u = 2 * s + d
                    w_copy(u, target).wait_recv()

                    @pl.when(distance(d) < n_pair - 1)
                    def _():
                        w_copy(u, target).start()

    def ready(d, base):
        return jnp.clip(base + LEAD * (n_pair - 1 - distance(d)), 0, steps)

    local = pltpu.make_async_copy(amp_ref.at[0], t_ref.at[i, rows_of(j)], loc_sem)
    local.start()
    mirror_copy(mirror, z).start()
    for step in range(1, n_pair):
        peer = lax.rem(i + step, n_pair)
        o_copy(peer, i).start()

    @pl.when(pos == 0)
    def _():
        for k in range(chunks):
            w8_load(k).start()
        row = lax.broadcasted_iota(jnp.int32, pick_ref.shape, 0)
        col = lax.broadcasted_iota(jnp.int32, pick_ref.shape, 1)
        hit = (row == (col // PAD) * rows + col % PAD) & (col % PAD < rows)
        pick_ref[...] = jnp.where(hit, 1.0, 0.0).astype(BF16)

    for k in range(slots):
        load_factors(k).start()

    @pl.when(pos == 0)
    def _():
        for k in range(early):
            squeeze(k)
        for k in range(early):
            send_units(k)

    local.wait()
    for step in range(1, n_pair):
        source = lax.rem(i + n_pair - step, n_pair)
        o_copy(i, source).wait_recv()
    for step in range(1, half):
        z_copy(base + lax.rem(z - base + step, half), z).start()
    c_copy(z, core).start()

    mirror_copy(z, mirror).wait_recv()
    for step in range(1, n_pair):
        peer = lax.rem(i + step, n_pair)
        m_copy(peer, i).start()

    @pl.when(pos == 0)
    def _():
        squeeze(early)

        @pl.loop(early, chunks)
        def _(k):
            @pl.when(k + 1 < chunks)
            def _():
                squeeze(k + 1)

            send_units(k)

    for step in range(1, n_pair):
        source = lax.rem(i + n_pair - step, n_pair)
        m_copy(i, source).wait_recv()
    for step in range(1, half):
        z_copy(base + lax.rem(z - base + step, half), mirror).start()
    c_copy(mirror, core).start()

    handle(lambda d: 0, lambda d: ready(d, STAGES[0]))
    for step in range(1, half):
        source = base + lax.rem(z - base + half - step, half)
        z_copy(z, source).wait_recv()
        c_copy(source, core).start()
    handle(lambda d: ready(d, STAGES[0]), lambda d: ready(d, STAGES[1]))
    for step in range(1, half):
        source = far + lax.rem(z - base + half - step, half)
        z_copy(z, source).wait_recv()
        c_copy(source, core).start()

    flip_ref[...] = jnp.zeros_like(flip_ref)
    part_ref[...] = jnp.zeros_like(part_ref)
    e_row = lax.broadcasted_iota(jnp.int32, (chunk * PAD, chunk * rows), 0)
    e_col = lax.broadcasted_iota(jnp.int32, (chunk * PAD, chunk * rows), 1)
    hit = (e_col == (e_row // PAD) * rows + e_row % PAD) & (e_row % PAD < rows)
    keep_ref[...] = jnp.where(hit, 1.0, 0.0).astype(BF16)

    for group in range(m):
        c_copy(group, 1 - core).wait_recv()

    def handled(d, k):
        value = jnp.maximum(
            ready(d, STAGES[2] + (k * PACE[0]) // PACE[1]), jnp.minimum((k + 1) * per // 2, steps)
        )
        return jnp.where(k < 0, ready(d, STAGES[1]), value)

    @pl.loop(0, chunks)
    def _(k):
        handle(lambda d: handled(d, k - 1), lambda d: handled(d, k))
        load_factors(k).wait()
        slot = lax.rem(k, slots)
        tight = w_ref[pl.ds(k * per, per)].reshape(chunk * rows, width)
        wide = jnp.dot(keep_ref[...], tight, preferred_element_type=F32).astype(BF16)
        for p in range(0, n_pair, 2):
            two = [
                jnp.dot(wide, t_ref[p + at], preferred_element_type=F32).reshape(chunk, PAD, width)
                for at in range(2)
            ]
            h_ref[:, p * PAD : (p + 2) * PAD, :] = jnp.concatenate(two, axis=1).astype(BF16)

        def add(g, totals):
            flip, part = totals
            flip = flip + lax.dot_general(
                f_ref[slot, 2 * g], h_ref[2 * g], (((1,), (1,)), ((), ())), preferred_element_type=F32
            )
            part = part + lax.dot_general(
                h_ref[2 * g + 1], f_ref[slot, 2 * g + 1], (((1,), (1,)), ((), ())), preferred_element_type=F32
            )
            return flip, part

        zeros = (jnp.zeros((block, n_pair * PAD), F32), jnp.zeros((n_pair * PAD, block), F32))
        flip, part = lax.fori_loop(0, chunk // 2, add, zeros, unroll=chunk // 2)
        flip_ref[...] += flip
        part_ref[...] += part

        @pl.when(k + slots < chunks)
        def _():
            load_factors(k + slots).start()

    send_ref[...] = (flip_ref[...].T + part_ref[...]).reshape(n_pair, PAD, block)
    ratio = n_aux // n_pair

    def r_copy(p, t, source, to):
        return pltpu.make_async_remote_copy(
            src_ref=send_ref.at[p], dst_ref=got_ref.at[source],
            send_sem=r_send.at[p * ratio + t], recv_sem=r_recv.at[source],
            device_id=to, device_id_type=MESH,
        )

    for p in range(n_pair):
        for t in range(ratio):
            column = i * ratio + t
            mine = (i == p) & (j == column)

            @pl.when(mine)
            def _():
                got_ref[j] = send_ref[p]

            @pl.when(jnp.logical_not(mine))
            def _():
                r_copy(p, t, j, (jnp.int32(p), column)).start()

    def cut(values):
        out = values[..., :columns]
        for at in range(1, n_aux):
            out = jnp.where(j == at, values[..., at * columns : (at + 1) * columns], out)
        return out

    hole = jnp.zeros((PAD, columns), F32)
    mine = jnp.zeros((PAD, columns), F32)
    for p in range(n_pair):
        slab = cut(t_ref[p, 0:16, :].astype(F32)[:PAD])
        hole = hole + hole_ref[i, p] * slab
        mine = jnp.where(i == p, slab, mine)
    eps_cols = cut(eps_row_ref[...])
    a_at = lax.broadcasted_iota(jnp.int32, (PAD, columns), 0)
    eps_rows = jnp.zeros((PAD, columns), F32)
    for a in range(rows):
        eps_rows = jnp.where(a_at == a, eps_ref[a], eps_rows)
    denominator = (eps_rows + eps_cols - energy_ref[0])[:rows]
    fixed = driver_ref[0] + hole[:rows]

    column_owner = j // ratio
    for source in range(n_aux):
        @pl.when(jnp.logical_not((column_owner == i) & (j == source)))
        def _():
            r_copy(0, 0, source, (i, j)).wait_recv()

    total = got_ref[0]
    for source in range(1, n_aux):
        total = total + got_ref[source]
    particle = total[:, :columns]
    for t in range(1, ratio):
        particle = jnp.where(lax.rem(j, ratio) == t, total[:, t * columns : (t + 1) * columns], particle)
    residual = fixed + particle[:rows]
    res_ref[0] = residual
    new_ref[0] = mine[:rows] - residual / denominator

    for p in range(n_pair):
        for t in range(ratio):
            column = i * ratio + t

            @pl.when(jnp.logical_not((i == p) & (j == column)))
            def _():
                r_copy(p, t, j, (jnp.int32(p), column)).wait_send()
    mirror_copy(mirror, z).wait_send()
    for step in range(1, n_pair):
        peer = lax.rem(i + step, n_pair)
        o_copy(peer, i).wait_send()
        m_copy(peer, i).wait_send()
    for step in range(1, half):
        target = base + lax.rem(z - base + step, half)
        z_copy(target, z).wait_send()
        z_copy(target, mirror).wait_send()
    for group in range(m):
        c_copy(group, core).wait_send()

    for d in range(2):
        @pl.when(distances[d] < n_pair - 1)
        def _():
            @pl.loop(0, steps)
            def _(s):
                w_copy(2 * s + d, targets[d]).wait_send()


def per_device(n_pair, n_aux, amplitudes, factors, hole_weights, driver, eps_vir, pair_energy):
    rows, columns = driver.shape[1:]
    depth, block, width = factors.shape
    own_rows = amplitudes.shape[1]
    chunk = min(32, depth)
    unit = chunk // SPLIT
    chunks = depth // chunk
    units = depth // unit
    slots = min(8, chunks)
    early = min(1, chunks)
    m = n_aux // 2
    half = m // 2
    ratio = n_aux // n_pair
    vmem = pl.BlockSpec(memory_space=pltpu.VMEM)
    smem = pl.BlockSpec(memory_space=pltpu.SMEM)
    hbm = pl.BlockSpec(memory_space=pl.ANY)
    dma = pltpu.SemaphoreType.DMA
    return pl.pallas_call(
        functools.partial(kernel, n_pair, n_aux, rows, columns, chunk, unit, slots, early),
        out_shape=(
            jax.ShapeDtypeStruct(driver.shape, F32),
            jax.ShapeDtypeStruct(driver.shape, F32),
        ),
        in_specs=[hbm, hbm, smem, vmem, smem, vmem, smem],
        out_specs=(vmem, vmem),
        scratch_shapes=[
            pltpu.VMEM((n_pair, n_aux * own_rows, width), BF16),
            pltpu.VMEM((chunks, chunk, PAD, width), BF16),
            pltpu.VMEM((units, unit * rows, width), BF16),
            pltpu.VMEM((slots, chunk, block, width), BF16),
            pltpu.VMEM((chunk, n_pair * PAD, width), BF16),
            pltpu.VMEM((n_pair * PAD, block), F32),
            pltpu.VMEM((block, n_pair * PAD), F32),
            pltpu.VMEM((n_pair, PAD, block), F32),
            pltpu.VMEM((n_aux, PAD, block), F32),
            pltpu.VMEM((chunk * PAD, chunk * rows), BF16),
            pltpu.VMEM((chunk * rows, chunk * PAD), BF16),
            dma((slots,)),
            dma,
            dma((chunks,)),
            dma((n_pair,)),
            dma((n_pair,)),
            dma,
            dma,
            dma((n_pair,)),
            dma((n_pair,)),
            dma((m,)),
            dma((m,)),
            dma((m,)),
            dma((m,)),
            dma((units,)),
            dma((units,)),
            dma((n_pair * ratio,)),
            dma((n_aux,)),
        ],
        compiler_params=pltpu.CompilerParams(has_side_effects=True, vmem_limit_bytes=60 * 1024 * 1024),
    )(amplitudes, factors, hole_weights, driver, eps_vir, eps_vir.reshape(1, width), pair_energy)


def solution(mesh):
    return jax.shard_map(
        functools.partial(per_device, mesh.shape["pair"], mesh.shape["aux"]),
        mesh=mesh,
        in_specs=(
            P("pair", "aux", None),
            P("aux", "pair", None),
            P(),
            P("pair", None, "aux"),
            P(),
            P("pair"),
        ),
        out_specs=(P("pair", None, "aux"), P("pair", None, "aux")),
        check_vma=False,
    )
```

time: 116 us -> 78.2 us (0.67)
  Pallas kernels: 97.4 us -> 72.8 us
  local copies, waits for them, and re-layouts: 13.5 us -> 3.78 us
  other arithmetic: 3.34 us -> 0 us
    pallas_call x1, Pallas kernels: 97.4 us -> 72.8 us  [per_device(): pl.pallas_call(functools.partial(kernel, n_pair, n_aux, rows, columns, ch...]
    reshape x1 -> x0, local copies, waits for them, and re-layouts: 6.4 us -> none  [per_device(): window = factors[:, :rows, :].reshape(chunks, chunk * rows, width)]
    slice x5 -> x0, local copies, waits for them, and re-layouts: 5.83 us -> none  [the longest x1 4.4 us: per_device(): window = factors[:, :rows, :].reshape(chunks, chunk * rows, width)]
    sub x1 -> x0, other arithmetic: 3.26 us -> none  [per_device(): return (residual, amp_cols - residual / denominator)]
    pallas_call x0 -> x2, local copies, waits for them, and re-layouts: none -> 2.51 us  [per_device(): pl.pallas_call(functools.partial(kernel, n_pair, n_aux, rows, columns, ch...]
where the time goes in v1:
time: 78.2 us; the launch traced here: 77.9 us
  Pallas kernels  72.8 us (93%)
  local copies, waits for them, and re-layouts  3.78 us (5%)
  between operations  1.29 us (2%)
    pallas_call x1, Pallas kernels, per_device(): pl.pallas_call(functools.partial(kernel, n_pair, n_aux, rows, columns, ch...  72.8 us
    pallas_call x2, local copies, waits for them, and re-layouts, per_device(): pl.pallas_call(functools.partial(kernel, n_pair, n_aux, rows, columns, ch...  2.51 us

profile of v1, /device:TPU:13, one launch (start us, length us, event | category | flops | bytes accessed | tf_op | source)
XLA Modules:
  0.0 77.9 jit_solution(7341039376904743399)
XLA Ops:
  1.3 1.3 %copy.8.driver_ref = f32[1,6,64]{2,1,0:T(8,128)} copy(f32[1,6,64]{2,0,1:T(1,128)} %param.9) | data formatting | bytes 3072 | tf_op args[3]
  2.5 72.8 %shard_map.77 = (f32[1,6,64]{2,1,0:T(8,128)}, f32[1,6,64]{2,1,0:T(8,128)}) custom-call(bf16[1,64,512]{2,1,0:T(8,128)(2,1)} %amp_ref.1, bf16[512,128,512]{2,1,0:T(8,128)(2,1)} %fac_ref.1, f32[4,4]{1,0:T(4,128)} %hole_ref.1, f32[1,6,64]{2,1,0:T(8,128)} %copy.8.driver_ref, f32[512]{0:T(512)} %eps_ref.1, f32[1,512]{1,0:T(1,128)} %bitcast.1, f32[1]{0:T(128)S(6)} %copy.11.energy_ref), custom_call_target="tpu_custom_call" | custom-call | tf_op jit(solution)/shard_map/pallas_call | solution.py:393
  75.4 1.3 %copy.9 = f32[1,6,64]{2,0,1:T(1,128)} copy(f32[1,6,64]{2,1,0:T(8,128)} %get-tuple-element.2) | data formatting | bytes 3072 | tf_op jit(solution)/shard_map/pallas_call | solution.py:393
  76.7 1.3 %copy.10 = f32[1,6,64]{2,0,1:T(1,128)} copy(f32[1,6,64]{2,1,0:T(8,128)} %get-tuple-element.3) | data formatting | bytes 3072 | tf_op jit(solution)/shard_map/pallas_call | solution.py:393

commit v2 on v1

--- a/solution.py
+++ b/solution.py
@@ -12,9 +12,10 @@
 BF16 = jnp.bfloat16
 PAD = 8
 SPLIT = 2
-LEAD = 2
-STAGES = (-2, 1, 2)
-PACE = (9, 10)
+LEAD = 3
+STAGES = (-2, -1, 0)
+PACE = (1, 1)
+GRANT = 60 * 1024 * 1024
 
 
 def ring_order(n):
@@ -45,9 +46,9 @@
 def kernel(
     n_pair, n_aux, rows, columns, chunk, unit, slots, early,
     amp_ref, fac_ref, hole_ref, driver_ref, eps_ref, eps_row_ref, energy_ref,
-    res_ref, new_ref,
-    t_ref, w8_ref, w_ref, f_ref, h_ref, part_ref, flip_ref, send_ref, got_ref, keep_ref, pick_ref,
-    f_sem, loc_sem, w8_sem, o_send, o_recv, y_send, y_recv, m_send, m_recv,
+    out_ref,
+    t_ref, w8_ref, w_ref, f_ref, h_ref, part_ref, flip_ref, send_ref, got_ref, keep_ref, pick_ref, d_ref,
+    f_sem, loc_sem, d_sem, w8_sem, o_send, o_recv, y_send, y_recv, m_send, m_recv,
     z_send, z_recv, c_send, c_recv, w_send, w_recv, r_send, r_recv,
 ):
     width = amp_ref.shape[2]
@@ -171,29 +172,45 @@
 
     local = pltpu.make_async_copy(amp_ref.at[0], t_ref.at[i, rows_of(j)], loc_sem)
     local.start()
+    driver_load = pltpu.make_async_copy(driver_ref, d_ref, d_sem)
+    driver_load.start()
+
+    @pl.when(pos == 0)
+    def _():
+        for k in range(chunks):
+            w8_load(k).start()
+
+    barrier = pltpu.get_barrier_semaphore()
+    friends = [(lax.rem(i + step, n_pair), j) for step in range(1, n_pair)]
+    friends += [(i, (base + lax.rem(z - base + step, half)) * 2 + core) for step in range(1, half)]
+    friends += [(i, mirror * 2 + core), (i, z * 2 + 1 - core)]
+    for friend in friends:
+        pl.semaphore_signal(barrier, inc=1, device_id=friend, device_id_type=MESH)
+
+    @pl.when(pos == 0)
+    def _():
+        row = lax.broadcasted_iota(jnp.int32, pick_ref.shape, 0)
+        col = lax.broadcasted_iota(jnp.int32, pick_ref.shape, 1)
+        hit = (row == (col // PAD) * rows + col % PAD) & (col % PAD < rows)
+        pick_ref[...] = jnp.where(hit, 1.0, 0.0).astype(BF16)
+        for k in range(early):
+            squeeze(k)
+
+    pl.semaphore_wait(barrier, len(friends))
+
     mirror_copy(mirror, z).start()
     for step in range(1, n_pair):
         peer = lax.rem(i + step, n_pair)
         o_copy(peer, i).start()
 
-    @pl.when(pos == 0)
-    def _():
-        for k in range(chunks):
-            w8_load(k).start()
-        row = lax.broadcasted_iota(jnp.int32, pick_ref.shape, 0)
-        col = lax.broadcasted_iota(jnp.int32, pick_ref.shape, 1)
-        hit = (row == (col // PAD) * rows + col % PAD) & (col % PAD < rows)
-        pick_ref[...] = jnp.where(hit, 1.0, 0.0).astype(BF16)
-
-    for k in range(slots):
-        load_factors(k).start()
 
     @pl.when(pos == 0)
     def _():
         for k in range(early):
-            squeeze(k)
-        for k in range(early):
             send_units(k)
+
+    for k in range(slots):
+        load_factors(k).start()
 
     local.wait()
     for step in range(1, n_pair):
@@ -328,7 +345,8 @@
     for a in range(rows):
         eps_rows = jnp.where(a_at == a, eps_ref[a], eps_rows)
     denominator = (eps_rows + eps_cols - energy_ref[0])[:rows]
-    fixed = driver_ref[0] + hole[:rows]
+    driver_load.wait()
+    fixed = jnp.concatenate([d_ref[a] for a in range(rows)], axis=0) + hole[:rows]
 
     column_owner = j // ratio
     for source in range(n_aux):
@@ -343,8 +361,10 @@
     for t in range(1, ratio):
         particle = jnp.where(lax.rem(j, ratio) == t, total[:, t * columns : (t + 1) * columns], particle)
     residual = fixed + particle[:rows]
-    res_ref[0] = residual
-    new_ref[0] = mine[:rows] - residual / denominator
+    updated = mine[:rows] - residual / denominator
+    for a in range(rows):
+        out_ref[a] = residual[a : a + 1]
+        out_ref[rows + a] = updated[a : a + 1]
 
     for p in range(n_pair):
         for t in range(ratio):
@@ -390,14 +410,11 @@
     smem = pl.BlockSpec(memory_space=pltpu.SMEM)
     hbm = pl.BlockSpec(memory_space=pl.ANY)
     dma = pltpu.SemaphoreType.DMA
-    return pl.pallas_call(
+    out = pl.pallas_call(
         functools.partial(kernel, n_pair, n_aux, rows, columns, chunk, unit, slots, early),
-        out_shape=(
-            jax.ShapeDtypeStruct(driver.shape, F32),
-            jax.ShapeDtypeStruct(driver.shape, F32),
-        ),
-        in_specs=[hbm, hbm, smem, vmem, smem, vmem, smem],
-        out_specs=(vmem, vmem),
+        out_shape=jax.ShapeDtypeStruct((2 * rows, 1, columns), F32),
+        in_specs=[hbm, hbm, smem, hbm, smem, vmem, smem],
+        out_specs=vmem,
         scratch_shapes=[
             pltpu.VMEM((n_pair, n_aux * own_rows, width), BF16),
             pltpu.VMEM((chunks, chunk, PAD, width), BF16),
@@ -410,7 +427,9 @@
             pltpu.VMEM((n_aux, PAD, block), F32),
             pltpu.VMEM((chunk * PAD, chunk * rows), BF16),
             pltpu.VMEM((chunk * rows, chunk * PAD), BF16),
+            pltpu.VMEM((rows, 1, columns), F32),
             dma((slots,)),
+            dma,
             dma,
             dma((chunks,)),
             dma((n_pair,)),
@@ -428,8 +447,12 @@
             dma((n_pair * ratio,)),
             dma((n_aux,)),
         ],
-        compiler_params=pltpu.CompilerParams(has_side_effects=True, vmem_limit_bytes=60 * 1024 * 1024),
-    )(amplitudes, factors, hole_weights, driver, eps_vir, eps_vir.reshape(1, width), pair_energy)
+        compiler_params=pltpu.CompilerParams(collective_id=0, has_side_effects=True, vmem_limit_bytes=GRANT),
+    )(
+        amplitudes, factors, hole_weights, jnp.swapaxes(driver, 0, 1),
+        eps_vir, eps_vir.reshape(1, width), pair_energy,
+    )
+    return jnp.swapaxes(out[:rows], 0, 1), jnp.swapaxes(out[rows:], 0, 1)
 
 
 def solution(mesh):

time: 78.2 us -> 65.6 us (0.84)
  Pallas kernels: 72.8 us -> 62.8 us
  local copies, waits for them, and re-layouts: 3.78 us -> 1.26 us
    pallas_call x1, Pallas kernels: 72.8 us -> 62.8 us  [per_device(): pl.pallas_call(functools.partial(kernel, n_pair, n_aux, rows, columns, ch...]
    pallas_call x2 -> x0, local copies, waits for them, and re-layouts: 2.51 us -> none  [per_device(): pl.pallas_call(functools.partial(kernel, n_pair, n_aux, rows, columns, ch...]
    unnamed x1 -> x0, local copies, waits for them, and re-layouts: 1.27 us -> none
    transpose x0 -> x1, local copies, waits for them, and re-layouts: none -> 1.26 us  [per_device(): return (jnp.swapaxes(out[:rows], 0, 1), jnp.swapaxes(out[rows:], 0, 1))]
where the time goes in v2:
time: 65.6 us; the launch traced here: 65.3 us
  Pallas kernels  62.8 us (96%)
  between operations  1.29 us (2%)
  local copies, waits for them, and re-layouts  1.26 us (2%)
    pallas_call x1, Pallas kernels, per_device(): pl.pallas_call(functools.partial(kernel, n_pair, n_aux, rows, columns, ch...  62.8 us

profile of v2, /device:TPU:13, one launch (start us, length us, event | category | flops | bytes accessed | tf_op | source)
XLA Modules:
  0.0 65.3 jit_solution(17239569884657327990)
XLA Ops:
  1.3 62.8 %shard_map.77 = f32[12,1,64]{2,1,0:T(1,128)} custom-call(bf16[1,64,512]{2,1,0:T(8,128)(2,1)} %amp_ref.1, bf16[512,128,512]{2,1,0:T(8,128)(2,1)} %fac_ref.1, f32[4,4]{1,0:T(4,128)} %hole_ref.1, f32[6,1,64]{2,1,0:T(1,128)} %bitcast.7, f32[512]{0:T(512)} %eps_ref.1, f32[1,512]{1,0:T(1,128)} %bitcast.6, f32[1]{0:T(128)S(6)} %copy.8.energy_ref), custom_call_target="tpu_custom_call" | custom-call | tf_op jit(solution)/shard_map/pallas_call | solution.py:413
  64.0 1.3 %slice_bitcast_fusion = (f32[1,6,64]{2,0,1:T(1,128)}, f32[1,6,64]{2,0,1:T(1,128)}) fusion(f32[12,1,64]{2,1,0:T(1,128)} %shard_map.77), kind=kLoop, calls=%fused_computation | loop fusion | bytes 6144 | tf_op jit(solution)/shard_map/transpose | solution.py:455
